TPU v7x, 32 devices: a whole 2x2x4 slice. The times are simulated.
32 devices in a mesh: beam: 2 (over x), pulse: 16 (over z, y, core).
Axes of the slice: x: 2, y: 2, z: 4, core: 2. Of those that a mesh axis runs over, the one named last changes fastest.
Arguments:
- echoes: float32 [2, 4096, 1536], P(None, 'pulse', 'beam'), parts along dimension 2, may hold values from -6 to 6
- guard_gates: int32 [1], replicated, may hold values from 1 to 4
- train_gates: int32 [1], replicated, may hold values from 4 to 16
Outputs:
- powers: float32 [4096, 1536], P('pulse', 'beam'), parts along dimension 1
- statistic: float32 [4096, 1536], P('pulse', 'beam'), parts along dimension 1
There are 2 independent parts, one for each index of `beam`. A program takes and returns all parts, laid end to end along the dimension named above; an argument that names none is the same for every part. Nothing has to cross between parts.
All inputs are finite; a program needn't handle non-finite values.
Results may differ from a plain program's by a relative error of at most 0.0003.
Values sent between devices are 32-bit elements; how exact they have to be, the bound alone decides.
A program may use at most 192 MiB of HBM per device.

v0:
```python
import functools

import jax
import jax.numpy as jnp
import numpy as np
from jax import lax
from jax.experimental import pallas as pl
from jax.experimental.pallas import tpu as pltpu
from jax.sharding import PartitionSpec as P

PULSES = 4096
GUARD_BINS = 2
TRAIN_BINS = 4


TWO_PI = 6.283185307179586


def padded_2(cells, sides, width):
    for axis, dim in sides:
        count = lax.axis_size(axis)
        head = lax.slice_in_dim(cells, 0, width, axis=dim)
        tail = lax.slice_in_dim(cells, cells.shape[dim] - width, cells.shape[dim], axis=dim)
        cells = jnp.concatenate(
            [
                lax.ppermute(tail, axis, [(i, (i + 1) % count) for i in range(count)]),
                cells,
                lax.ppermute(head, axis, [((i + 1) % count, i) for i in range(count)]),
            ],
            axis=dim,
        )
    return cells


def small_tables(count):
    index_row = jnp.arange(count, dtype=jnp.int32)
    phases = (index_row[:, None] * index_row[None, :] % count).astype(jnp.float32) * (
        TWO_PI / count
    )
    return (jnp.cos(phases), jnp.sin(phases))


def product(left, right):
    return jnp.dot(left, right, precision=lax.Precision.HIGHEST, preferred_element_type=jnp.float32)


def factored_powers(samples):
    width = samples.shape[2]
    bit_count = PULSES.bit_length() - 1
    first_radix = 2 ** (bit_count // 2)
    second_radix = PULSES // first_radix
    cos_first, sin_first = small_tables(first_radix)
    real_in = samples[0].reshape(first_radix, second_radix * width)
    imag_in = samples[1].reshape(first_radix, second_radix * width)
    real_one = (product(cos_first, real_in) + product(sin_first, imag_in)).reshape(
        first_radix, second_radix, width
    )
    imag_one = (product(cos_first, imag_in) - product(sin_first, real_in)).reshape(
        first_radix, second_radix, width
    )
    first_ids = jnp.arange(first_radix, dtype=jnp.int32)
    second_ids = jnp.arange(second_radix, dtype=jnp.int32)
    twist = (first_ids[:, None] * second_ids[None, :] % PULSES).astype(jnp.float32) * (
        TWO_PI / PULSES
    )
    twist_cos = jnp.cos(twist)[:, :, None]
    twist_sin = jnp.sin(twist)[:, :, None]
    real_two = twist_cos * real_one + twist_sin * imag_one
    imag_two = twist_cos * imag_one - twist_sin * real_one
    real_two = jnp.transpose(real_two, (1, 0, 2)).reshape(second_radix, first_radix * width)
    imag_two = jnp.transpose(imag_two, (1, 0, 2)).reshape(second_radix, first_radix * width)
    cos_second, sin_second = small_tables(second_radix)
    scale_factor = 1.0 / jnp.sqrt(jnp.float32(PULSES))
    real_out = (product(cos_second, real_two) + product(sin_second, imag_two)) * scale_factor
    imag_out = (product(cos_second, imag_two) - product(sin_second, real_two)) * scale_factor
    result = real_out * real_out + imag_out * imag_out
    return result.reshape(PULSES, width)


def generic_shards(echoes, guard_gates, train_gates):
    devices_count = lax.axis_size("pulse")
    bins_local = PULSES // devices_count
    gates_count = echoes.shape[2]
    columns = factored_powers(
        lax.all_to_all(echoes, "pulse", split_axis=2, concat_axis=1, tiled=True)
    )
    powers = lax.all_to_all(columns, "pulse", split_axis=0, concat_axis=1, tiled=True)
    reach = GUARD_BINS + TRAIN_BINS
    padded = padded_2(powers, (("pulse", 0),), reach)
    doppler_sum = jnp.zeros_like(powers)
    for shift_bins in range(GUARD_BINS + 1, reach + 1):
        above = padded[reach + shift_bins : reach + shift_bins + bins_local]
        below = padded[reach - shift_bins : reach - shift_bins + bins_local]
        doppler_sum = doppler_sum + above + below
    guard_width = guard_gates[0]
    train_width = train_gates[0]
    gate_ids = jnp.arange(gates_count, dtype=jnp.int32)
    offsets = jnp.abs(gate_ids[:, None] - gate_ids[None, :])
    band = ((offsets > guard_width) & (offsets <= guard_width + train_width)).astype(jnp.float32)
    range_sum = jnp.dot(
        powers, band, precision=lax.Precision.HIGHEST, preferred_element_type=jnp.float32
    )
    range_count = jnp.sum(band, axis=0)
    noise_level = (range_sum + doppler_sum) / (range_count[None, :] + 2.0 * TRAIN_BINS)
    statistic = powers / (noise_level + 1.0)
    return (powers, statistic)


LANES = 128
ROWS = 8
HIGHEST = lax.Precision.HIGHEST


def butterflies(cells):
    count = len(cells)
    if count == 1:
        return cells
    even = butterflies(cells[0::2])
    odd = butterflies(cells[1::2])
    low, high = [], []
    for k in range(count // 2):
        re, im = odd[k]
        if 4 * k == count:
            re, im = im, -re
        elif k:
            c, s = np.cos(2 * np.pi * k / count), np.sin(2 * np.pi * k / count)
            c, s = np.float32(c), np.float32(s)
            re, im = c * re + s * im, c * im - s * re
        low.append((even[k][0] + re, even[k][1] + im))
        high.append((even[k][0] - re, even[k][1] - im))
    return low + high


def swap_digits(rows, width):
    count = len(rows)
    lane = lax.broadcasted_iota(jnp.int32, rows[0][0].shape, 1)
    bit = 1
    while bit < count:
        step = bit * width
        keep = (lane // step) % 2 == 0 if step < LANES else None
        for f in range(count):
            if f & bit:
                continue
            first, second = rows[f], rows[f | bit]
            if step < LANES:
                new_first = [
                    jnp.where(keep, a, pltpu.roll(b, step, 1)) for a, b in zip(first, second)
                ]
                new_second = [
                    jnp.where(keep, pltpu.roll(a, LANES - step, 1), b)
                    for a, b in zip(first, second)
                ]
            else:
                hop = step // LANES
                new_first, new_second = list(first), list(second)
                for h in range(len(first)):
                    if h & hop:
                        new_first[h] = second[h ^ hop]
                    else:
                        new_second[h] = first[h ^ hop]
            rows[f], rows[f | bit] = new_first, new_second
        bit *= 2
    return rows


def split(values):
    high = values.astype(jnp.bfloat16)
    return high, (values - high.astype(jnp.float32)).astype(jnp.bfloat16)


def bf16_dot(left, right, dims=(((1,), (0,)), ((), ()))):
    return lax.dot_general(left, right, dims, preferred_element_type=jnp.float32)


def rows_of(picks, columns):
    return lax.dot_general(
        picks, columns, (((1,), (1,)), ((), ())),
        precision=HIGHEST, preferred_element_type=jnp.float32,
    )


def kernel(
    n, chunks, guard_ref, train_ref, x_any, high_any, low_any, cos_any, sin_any, perm_any,
    power_ref, stat_ref,
    sent, got, mixed, cells, landed, padded, edges,
    x_ref, table_high, table_low, twist_cos, twist_sin, perm_ref,
    send_one, recv_one, send_two, recv_two, send_edge, recv_edge, load,
):
    me = lax.axis_index("pulse")
    length, gates = x_ref.shape[1], x_ref.shape[2]
    part = gates // n // chunks
    halves = length // LANES
    barrier = pltpu.get_barrier_semaphore()
    for o in peer_order(n):
        pl.semaphore_signal(barrier, inc=1, device_id={"pulse": partner(me, o)})
    loads = [pltpu.make_async_copy(x_any.at[p], x_ref.at[p], load.at[p]) for p in range(2)]
    pairs = (
        (high_any, table_high), (low_any, table_low), (cos_any, twist_cos), (sin_any, twist_sin),
        (perm_any, perm_ref),
    )
    for i, (source, target) in enumerate(pairs):
        loads.append(pltpu.make_async_copy(source, target, load.at[2 + i]))
    for copy in loads:
        copy.start()
    for p in range(2):
        loads[p].wait()
        sent[:, :, p] = x_ref[p].T.reshape(n, chunks, part, length)
    pl.semaphore_wait(barrier, n - 1)

    def first_copy(c, o):
        peer = partner(me, o)
        return pltpu.make_async_remote_copy(
            src_ref=sent.at[peer, c], dst_ref=got.at[c, me],
            send_sem=send_one.at[c, o], recv_sem=recv_one.at[c, o],
            device_id={"pulse": peer},
        )

    def second_copy(c, o):
        peer = partner(me, o)
        return pltpu.make_async_remote_copy(
            src_ref=cells.at[peer, c], dst_ref=landed.at[me, c],
            send_sem=send_two.at[c, o], recv_sem=recv_two.at[c, o],
            device_id={"pulse": peer},
        )

    order = peer_order(n)
    for c in range(chunks):
        for o in order:
            first_copy(c, o).start()
    for c in range(chunks):
        got[c, me] = sent[me, c]
    for copy in loads[2:]:
        copy.wait()
    gate_row = lax.broadcasted_iota(jnp.int32, (gates, gates), 0)
    gate_col = lax.broadcasted_iota(jnp.int32, (gates, gates), 1)
    offsets = jnp.abs(gate_row - gate_col)
    guard, train = guard_ref[0], train_ref[0]
    inside = ((offsets > guard) & (offsets <= guard + train)).astype(jnp.float32)
    range_count = jnp.sum(inside, axis=0, keepdims=True)
    band = inside.astype(jnp.bfloat16)

    for c in range(chunks):
        for o in order:
            first_copy(c, o).wait_recv()
        for r in range(0, part, ROWS):
            for h in range(halves):
                lanes = slice(h * LANES, (h + 1) * LANES)
                spectra = butterflies(
                    [
                        (got[c, s, 0, r : r + ROWS, lanes], got[c, s, 1, r : r + ROWS, lanes])
                        for s in range(n)
                    ]
                )
                for f, (re, im) in enumerate(spectra):
                    tc, ts = twist_cos[f : f + 1, lanes], twist_sin[f : f + 1, lanes]
                    mixed[0, f, r : r + ROWS, lanes] = tc * re + ts * im
                    mixed[1, f, r : r + ROWS, lanes] = tc * im - ts * re
        high, low = split(mixed[...].reshape(2 * n * part, length))
        both = (
            bf16_dot(high, table_high[...])
            + bf16_dot(low, table_high[...])
            + bf16_dot(high, table_low[...])
        ).reshape(2, n * part, 2 * length)
        real = both[0, :, :length] + both[1, :, length:]
        imag = both[1, :, :length] - both[0, :, length:]
        power = (real * real + imag * imag).reshape(n, part, length)
        rows = [
            [power[f, :, h * LANES : (h + 1) * LANES] for h in range(halves)] for f in range(n)
        ]
        rows = swap_digits(rows, length // n)
        for d in range(n):
            for h in range(halves):
                cells[d, c, :, h * LANES : (h + 1) * LANES] = rows[d][h]
        for o in order:
            second_copy(c, o).start()
        landed[me, c] = cells[me, c]
    for c in range(chunks):
        for o in order:
            second_copy(c, o).wait_recv()

    columns = landed[...].reshape(gates, length)
    ends = jnp.concatenate([perm_ref[:ROWS], perm_ref[length - ROWS :]])
    ends = rows_of(ends, columns)
    edges[0] = ends[:ROWS]
    edges[1] = ends[ROWS:]
    above, below = lax.rem(me + 1, n), lax.rem(me + n - 1, n)
    tail_copy = pltpu.make_async_remote_copy(
        src_ref=edges.at[1], dst_ref=edges.at[2],
        send_sem=send_edge.at[0], recv_sem=recv_edge.at[0], device_id={"pulse": above},
    )
    head_copy = pltpu.make_async_remote_copy(
        src_ref=edges.at[0], dst_ref=edges.at[3],
        send_sem=send_edge.at[1], recv_sem=recv_edge.at[1], device_id={"pulse": below},
    )
    tail_copy.start()
    head_copy.start()
    powers = rows_of(perm_ref[...], columns)
    power_ref[...] = powers
    high, low = split(powers)
    range_sum = bf16_dot(high, band) + bf16_dot(low, band)
    padded[ROWS : ROWS + length] = powers

    def finish(first, last):
        total = range_sum[first:last]
        for d in range(GUARD_BINS + 1, GUARD_BINS + TRAIN_BINS + 1):
            for move in (d, -d):
                total = total + padded[ROWS + first + move : ROWS + last + move]
        noise = total / (range_count + 2.0 * TRAIN_BINS)
        stat_ref[first:last] = powers[first:last] / (noise + 1.0)

    finish(ROWS, length - ROWS)
    tail_copy.wait_recv()
    head_copy.wait_recv()
    padded[:ROWS] = edges[2]
    padded[ROWS + length :] = edges[3]
    finish(0, ROWS)
    finish(length - ROWS, length)
    tail_copy.wait_send()
    head_copy.wait_send()
    for c in range(chunks):
        for o in order:
            first_copy(c, o).wait_send()
            second_copy(c, o).wait_send()


def partner(me, offset):
    peer, bit = me, 1
    while bit <= offset:
        if offset & bit:
            peer = peer + bit * (1 - 2 * lax.rem(lax.div(me, bit), 2))
        bit *= 2
    return peer


def peer_order(n):
    return list(range(n - 1, 0, -1))


def tables(n, length):
    lane = np.arange(length)
    turn = 2 * np.pi * (np.outer(lane, lane) % length) / length
    both = np.concatenate([np.cos(turn), np.sin(turn)], axis=1).astype(np.float32)
    high = both.astype(jnp.bfloat16)
    low = (both - high.astype(np.float32)).astype(jnp.bfloat16)
    twist = 2 * np.pi * np.outer(np.arange(n), lane) / (n * length)
    scale = 1.0 / np.sqrt(n * length)
    perm = np.zeros((length, length), np.float32)
    width = length // n
    for f in range(n):
        for e in range(width):
            perm[f + n * e, f * width + e] = 1.0
    return (
        high, low,
        (np.cos(twist) * scale).astype(np.float32),
        (np.sin(twist) * scale).astype(np.float32),
        perm,
    )


def kernel_shards(echoes, guard_gates, train_gates):
    n = lax.axis_size("pulse")
    length, gates = echoes.shape[1], echoes.shape[2]
    chunks = CHUNKS if gates % (n * ROWS * CHUNKS) == 0 else 1
    part = gates // n // chunks
    smem = pl.BlockSpec(memory_space=pltpu.SMEM)
    vmem = pl.BlockSpec(memory_space=pltpu.VMEM)
    out = jax.ShapeDtypeStruct((length, gates), jnp.float32)
    dma = pltpu.SemaphoreType.DMA
    results = pl.pallas_call(
        functools.partial(kernel, n, chunks),
        out_shape=(out, out),
        in_specs=[smem, smem] + [pl.BlockSpec(memory_space=pl.ANY)] * 6,
        out_specs=(vmem, vmem),
        scratch_shapes=[
            pltpu.VMEM((n, chunks, 2, part, length), jnp.float32),
            pltpu.VMEM((chunks, n, 2, part, length), jnp.float32),
            pltpu.VMEM((2, n, part, length), jnp.float32),
            pltpu.VMEM((n, chunks, part, length), jnp.float32),
            pltpu.VMEM((n, chunks, part, length), jnp.float32),
            pltpu.VMEM((length + 2 * ROWS, gates), jnp.float32),
            pltpu.VMEM((4, ROWS, gates), jnp.float32),
            pltpu.VMEM(echoes.shape, jnp.float32),
            pltpu.VMEM((length, 2 * length), jnp.bfloat16),
            pltpu.VMEM((length, 2 * length), jnp.bfloat16),
            pltpu.VMEM((n, length), jnp.float32),
            pltpu.VMEM((n, length), jnp.float32),
            pltpu.VMEM((length, length), jnp.float32),
            dma((chunks, n)), dma((chunks, n)), dma((chunks, n)), dma((chunks, n)),
            dma((2,)), dma((2,)), dma((7,)),
        ],
        compiler_params=pltpu.CompilerParams(
            collective_id=0, has_side_effects=True, vmem_limit_bytes=20 * 2**20
        ),
    )(guard_gates, train_gates, *(pltpu.with_memory_space_constraint(t, pltpu.HBM) for t in (echoes, *(jnp.asarray(t) for t in tables(n, length)))))
    return pl.pallas_call(
        write_out,
        out_shape=(out, out),
        in_specs=[vmem] * 2,
        out_specs=(pl.BlockSpec(memory_space=pl.ANY),) * 2,
        scratch_shapes=[dma((2,))],
        compiler_params=pltpu.CompilerParams(vmem_limit_bytes=8 * 2**20),
    )(*results)


def write_out(power_in, stat_in, power_out, stat_out, done):
    copies = [
        pltpu.make_async_copy(power_in, power_out, done.at[0]),
        pltpu.make_async_copy(stat_in, stat_out, done.at[1]),
    ]
    for copy in copies:
        copy.start()
    for copy in copies:
        copy.wait()


CHUNKS = 2


def shards(echoes, guard_gates, train_gates):
    n = lax.axis_size("pulse")
    length, gates = echoes.shape[1], echoes.shape[2]
    fits = length % LANES == 0 and length % n == 0 and n > 2 and gates % (n * ROWS) == 0
    fits = fits and n & (n - 1) == 0 and length & (length - 1) == 0 and LANES % (length // n) == 0
    if fits and GUARD_BINS + TRAIN_BINS <= ROWS:
        return kernel_shards(echoes, guard_gates, train_gates)
    return generic_shards(echoes, guard_gates, train_gates)


def solution(mesh):
    return jax.shard_map(
        shards,
        mesh=mesh,
        in_specs=(P(None, "pulse", "beam"), P(), P()),
        out_specs=(P("pulse", "beam"), P("pulse", "beam")),
        check_vma=False,
    )
```

profile of v0, /device:TPU:0, one launch (start us, length us, event | category | flops | bytes accessed | tf_op | source)
XLA Modules:
  0.0 66.9 jit_solution(16797634574192058326)
XLA Ops:
  1.9 63.8 %shard_map.95 = (f32[256,768]{1,0:T(8,128)S(1)}, f32[256,768]{1,0:T(8,128)S(1)}) custom-call(s32[1]{0:T(128)S(6)} %copy.10.guard_ref, s32[1]{0:T(128)S(6)} %copy.11.train_ref, f32[2,256,768]{2,1,0:T(8,128)} %x_any.1, bf16[256,512]{1,0:T(8,128)(2,1)} %constant.10.clone.high_any, bf16[256,512]{1,0:T(8,128)(2,1)} %constant.11.clone.low_any, ...), custom_call_target="tpu_custom_call" | custom-call | tf_op jit(solution)/shard_map/pallas_call | solution.py:369
  65.7 1.2 %shard_map.96 = (f32[256,768]{1,0:T(8,128)}, f32[256,768]{1,0:T(8,128)}) custom-call(f32[256,768]{1,0:T(8,128)S(1)} %get-tuple-element.4.power_in, f32[256,768]{1,0:T(8,128)S(1)} %get-tuple-element.5.stat_in), custom_call_target="tpu_custom_call" | custom-call | tf_op jit(solution)/shard_map/pallas_call | solution.py:395
where the time goes:
time: 67 us; the launch traced here: 66.9 us
  Pallas kernels  65 us (97%)
  between operations  1.93 us (3%)
    pallas_call x1, Pallas kernels, kernel_shards(): pl.pallas_call(functools.partial(kernel, n, chunks), out_shape=(out, out)...  63.8 us

commit v1 on v0

--- a/solution.py
+++ b/solution.py
@@ -172,86 +172,142 @@
     return lax.dot_general(left, right, dims, preferred_element_type=jnp.float32)
 
 
-def rows_of(picks, columns):
-    return lax.dot_general(
-        picks, columns, (((1,), (1,)), ((), ())),
-        precision=HIGHEST, preferred_element_type=jnp.float32,
-    )
+def inner_flag(me, n):
+    plane = lax.div(me, PLANE)
+    return lax.rem(lax.div(plane + 1, 2), 2)
+
+
+def partner(me, offset):
+    peer, bit = me, 1
+    while bit <= offset:
+        if offset & bit:
+            peer = peer + bit * (1 - 2 * lax.rem(lax.div(me, bit), 2))
+        bit *= 2
+    return peer
+
+
+def peer_orders(n):
+    ascending = list(range(1, n))
+    if n != PLANES * PLANE:
+        return ascending, ascending
+    hops = [[plane * PLANE + own for own in range(PLANE)] for plane in range(PLANES)]
+    own = hops[0][1:]
+    return hops[1] + hops[2] + hops[3] + own, hops[3] + hops[2] + hops[1] + own
 
 
 def kernel(
-    n, chunks, guard_ref, train_ref, x_any, high_any, low_any, cos_any, sin_any, perm_any,
-    power_ref, stat_ref,
-    sent, got, mixed, cells, landed, padded, edges,
-    x_ref, table_high, table_low, twist_cos, twist_sin, perm_ref,
-    send_one, recv_one, send_two, recv_two, send_edge, recv_edge, load,
+    n, chunks, x_any, high_any, low_any, cos_any, sin_any,
+    power_ref, total_ref,
+    sent, got, mixed, cells, landed, halo_out, halo_in, near_ref,
+    x_ref, table_high, table_low, twist_cos, twist_sin,
+    send_one, recv_one, send_two, recv_two, send_halo, recv_halo, load, ready,
 ):
     me = lax.axis_index("pulse")
     length, gates = x_ref.shape[1], x_ref.shape[2]
-    part = gates // n // chunks
+    wide = gates // chunks
+    part = wide // n
     halves = length // LANES
+    groups = part // ROWS
     barrier = pltpu.get_barrier_semaphore()
-    for o in peer_order(n):
-        pl.semaphore_signal(barrier, inc=1, device_id={"pulse": partner(me, o)})
-    loads = [pltpu.make_async_copy(x_any.at[p], x_ref.at[p], load.at[p]) for p in range(2)]
-    pairs = (
-        (high_any, table_high), (low_any, table_low), (cos_any, twist_cos), (sin_any, twist_sin),
-        (perm_any, perm_ref),
-    )
-    for i, (source, target) in enumerate(pairs):
-        loads.append(pltpu.make_async_copy(source, target, load.at[2 + i]))
+    for k in range(1, n):
+        @pl.when(me + k < n)
+        def _():
+            pl.semaphore_signal(barrier, inc=1, device_id={"pulse": lax.rem(me + k, n)})
+    loads = []
+    for c in range(chunks):
+        for p in range(2):
+            lanes = slice(c * wide, (c + 1) * wide)
+            loads.append((x_any.at[p, :, lanes], x_ref.at[p, :, lanes]))
+    loads += [
+        (cos_any, twist_cos), (sin_any, twist_sin), (high_any, table_high), (low_any, table_low),
+    ]
+    loads = [pltpu.make_async_copy(*pair, load.at[i]) for i, pair in enumerate(loads)]
     for copy in loads:
         copy.start()
-    for p in range(2):
-        loads[p].wait()
-        sent[:, :, p] = x_ref[p].T.reshape(n, chunks, part, length)
-    pl.semaphore_wait(barrier, n - 1)
-
-    def first_copy(c, o):
-        peer = partner(me, o)
+
+    @pl.when(me > 0)
+    def _():
+        pl.semaphore_wait(barrier, me)
+
+    for k in range(1, n):
+        @pl.when(me >= k)
+        def _():
+            pl.semaphore_signal(
+                ready.at[me], inc=1, device_id={"pulse": lax.rem(me + n - k, n)}
+            )
+
+    def fill(c):
+        for p in range(2):
+            loads[2 * c + p].wait()
+            block = x_ref[p, :, c * wide : (c + 1) * wide].T
+            sent[c, :, p] = block.reshape(n, part, length)
+
+    inner = inner_flag(me, n)
+    outer_order, inner_order = peer_orders(n)
+    peers = []
+    for a, b in zip(outer_order, inner_order):
+        if a == b:
+            peers.append((a, partner(me, a)))
+        else:
+            peers.append(
+                (
+                    a + inner * (b - a),
+                    (1 - inner) * partner(me, a) + inner * partner(me, b),
+                )
+            )
+
+    def first_copy(c, o, peer):
         return pltpu.make_async_remote_copy(
-            src_ref=sent.at[peer, c], dst_ref=got.at[c, me],
+            src_ref=sent.at[c, peer], dst_ref=got.at[c, me],
             send_sem=send_one.at[c, o], recv_sem=recv_one.at[c, o],
             device_id={"pulse": peer},
         )
 
-    def second_copy(c, o):
-        peer = partner(me, o)
+    def second_copy(c, o, peer):
         return pltpu.make_async_remote_copy(
-            src_ref=cells.at[peer, c], dst_ref=landed.at[me, c],
+            src_ref=cells.at[c, peer], dst_ref=landed.at[c, me],
             send_sem=send_two.at[c, o], recv_sem=recv_two.at[c, o],
             device_id={"pulse": peer},
         )
 
-    order = peer_order(n)
+    def halo_copy(c, o, peer):
+        return pltpu.make_async_remote_copy(
+            src_ref=halo_out.at[c, peer], dst_ref=halo_in.at[c, me],
+            send_sem=send_halo.at[c, o], recv_sem=recv_halo.at[c, o],
+            device_id={"pulse": peer},
+        )
+
+    fill(0)
+    for o, peer in peers:
+        @pl.when(peer > me)
+        def _():
+            pl.semaphore_wait(ready.at[peer], 1)
+
+        first_copy(0, o, peer).start()
+    for c in range(1, chunks):
+        fill(c)
+        for o, peer in peers:
+            first_copy(c, o, peer).start()
     for c in range(chunks):
-        for o in order:
-            first_copy(c, o).start()
-    for c in range(chunks):
-        got[c, me] = sent[me, c]
-    for copy in loads[2:]:
+        got[c, me] = sent[c, me]
+    for copy in loads[2 * chunks :]:
         copy.wait()
-    gate_row = lax.broadcasted_iota(jnp.int32, (gates, gates), 0)
-    gate_col = lax.broadcasted_iota(jnp.int32, (gates, gates), 1)
-    offsets = jnp.abs(gate_row - gate_col)
-    guard, train = guard_ref[0], train_ref[0]
-    inside = ((offsets > guard) & (offsets <= guard + train)).astype(jnp.float32)
-    range_count = jnp.sum(inside, axis=0, keepdims=True)
-    band = inside.astype(jnp.bfloat16)
-
-    for c in range(chunks):
-        for o in order:
-            first_copy(c, o).wait_recv()
+    bins = lax.broadcasted_iota(jnp.int32, (length, length), 0)
+    bins = jnp.abs(bins - lax.broadcasted_iota(jnp.int32, (length, length), 1))
+    inside = (bins > GUARD_BINS) & (bins <= GUARD_BINS + TRAIN_BINS)
+    near_ref[...] = inside.astype(jnp.float32).astype(jnp.bfloat16)
+
+    def spectra(c):
         for r in range(0, part, ROWS):
             for h in range(halves):
                 lanes = slice(h * LANES, (h + 1) * LANES)
-                spectra = butterflies(
+                spectrum = butterflies(
                     [
                         (got[c, s, 0, r : r + ROWS, lanes], got[c, s, 1, r : r + ROWS, lanes])
                         for s in range(n)
                     ]
                 )
-                for f, (re, im) in enumerate(spectra):
+                for f, (re, im) in enumerate(spectrum):
                     tc, ts = twist_cos[f : f + 1, lanes], twist_sin[f : f + 1, lanes]
                     mixed[0, f, r : r + ROWS, lanes] = tc * re + ts * im
                     mixed[1, f, r : r + ROWS, lanes] = tc * im - ts * re
@@ -267,160 +323,182 @@
         rows = [
             [power[f, :, h * LANES : (h + 1) * LANES] for h in range(halves)] for f in range(n)
         ]
-        rows = swap_digits(rows, length // n)
+        rows = swap_digits(rows, 1)
+        lane = lax.broadcasted_iota(jnp.int32, (part, LANES), 1)
         for d in range(n):
             for h in range(halves):
-                cells[d, c, :, h * LANES : (h + 1) * LANES] = rows[d][h]
-        for o in order:
-            second_copy(c, o).start()
-        landed[me, c] = cells[me, c]
+                cells[c, d, :, h * LANES : (h + 1) * LANES] = rows[d][h]
+        for d in range(n):
+            ends = jnp.where(
+                lane >= LANES - ROWS, rows[(d + n - 1) % n][halves - 1],
+                jnp.where(lane < ROWS, rows[(d + 1) % n][0], 0.0),
+            )
+            ends = pltpu.roll(ends, ROWS, 1, stride=2 * ROWS, stride_axis=0)
+            halo_out[c, d] = jnp.sum(ends.reshape(groups, ROWS, LANES), axis=1)
+
     for c in range(chunks):
-        for o in order:
-            second_copy(c, o).wait_recv()
-
-    columns = landed[...].reshape(gates, length)
-    ends = jnp.concatenate([perm_ref[:ROWS], perm_ref[length - ROWS :]])
-    ends = rows_of(ends, columns)
-    edges[0] = ends[:ROWS]
-    edges[1] = ends[ROWS:]
-    above, below = lax.rem(me + 1, n), lax.rem(me + n - 1, n)
-    tail_copy = pltpu.make_async_remote_copy(
-        src_ref=edges.at[1], dst_ref=edges.at[2],
-        send_sem=send_edge.at[0], recv_sem=recv_edge.at[0], device_id={"pulse": above},
-    )
-    head_copy = pltpu.make_async_remote_copy(
-        src_ref=edges.at[0], dst_ref=edges.at[3],
-        send_sem=send_edge.at[1], recv_sem=recv_edge.at[1], device_id={"pulse": below},
-    )
-    tail_copy.start()
-    head_copy.start()
-    powers = rows_of(perm_ref[...], columns)
-    power_ref[...] = powers
-    high, low = split(powers)
-    range_sum = bf16_dot(high, band) + bf16_dot(low, band)
-    padded[ROWS : ROWS + length] = powers
-
-    def finish(first, last):
-        total = range_sum[first:last]
+        for o, peer in peers:
+            first_copy(c, o, peer).wait_recv()
+        spectra(c)
+        for o, peer in peers:
+            halo_copy(c, o, peer).start()
+            second_copy(c, o, peer).start()
+        landed[c, me] = cells[c, me]
+        halo_in[c, me] = halo_out[c, me]
+
+    row = lax.broadcasted_iota(jnp.int32, (wide, LANES), 0)
+    lane = lax.broadcasted_iota(jnp.int32, (wide, LANES), 1)
+    mine = lane // (2 * ROWS) == row % ROWS
+    slot = lax.broadcasted_iota(jnp.int32, (2 * ROWS, LANES), 0)
+    lane = lax.broadcasted_iota(jnp.int32, (2 * ROWS, LANES), 1)
+    fold = (lane % (2 * ROWS) == slot).astype(jnp.float32).astype(jnp.bfloat16)
+    rest = jnp.zeros((ROWS, wide), jnp.float32)
+
+    for c in range(chunks):
+        for o, peer in peers:
+            halo_copy(c, o, peer).wait_recv()
+            second_copy(c, o, peer).wait_recv()
+        columns = slice(c * wide, (c + 1) * wide)
+        powers = landed[c].reshape(wide, length).T
+        power_ref[:, columns] = powers
+        high, low = split(powers)
+        total = bf16_dot(near_ref[...], high) + bf16_dot(near_ref[...], low)
+        packed = halo_in[c].reshape(n * groups, 1, LANES)
+        packed = jnp.broadcast_to(packed, (n * groups, ROWS, LANES)).reshape(wide, LANES)
+        high, low = split(jnp.where(mine, packed, 0.0))
+        last_dims = (((1,), (1,)), ((), ()))
+        halos = bf16_dot(fold, high, last_dims) + bf16_dot(fold, low, last_dims)
+        head = jnp.concatenate([halos[:ROWS], rest])
+        tail = jnp.concatenate([rest, halos[ROWS:]])
+        top, bottom = total[:ROWS], total[length - ROWS :]
         for d in range(GUARD_BINS + 1, GUARD_BINS + TRAIN_BINS + 1):
-            for move in (d, -d):
-                total = total + padded[ROWS + first + move : ROWS + last + move]
-        noise = total / (range_count + 2.0 * TRAIN_BINS)
-        stat_ref[first:last] = powers[first:last] / (noise + 1.0)
-
-    finish(ROWS, length - ROWS)
-    tail_copy.wait_recv()
-    head_copy.wait_recv()
-    padded[:ROWS] = edges[2]
-    padded[ROWS + length :] = edges[3]
-    finish(0, ROWS)
-    finish(length - ROWS, length)
-    tail_copy.wait_send()
-    head_copy.wait_send()
+            top = top + head[ROWS - d : 2 * ROWS - d]
+            bottom = bottom + tail[d : d + ROWS]
+        total_ref[:ROWS, columns] = top
+        total_ref[ROWS : length - ROWS, columns] = total[ROWS : length - ROWS]
+        total_ref[length - ROWS :, columns] = bottom
     for c in range(chunks):
-        for o in order:
-            first_copy(c, o).wait_send()
-            second_copy(c, o).wait_send()
-
-
-def partner(me, offset):
-    peer, bit = me, 1
-    while bit <= offset:
-        if offset & bit:
-            peer = peer + bit * (1 - 2 * lax.rem(lax.div(me, bit), 2))
-        bit *= 2
-    return peer
-
-
-def peer_order(n):
-    return list(range(n - 1, 0, -1))
+        for o, peer in peers:
+            first_copy(c, o, peer).wait_send()
+            halo_copy(c, o, peer).wait_send()
+            second_copy(c, o, peer).wait_send()
 
 
 def tables(n, length):
     lane = np.arange(length)
-    turn = 2 * np.pi * (np.outer(lane, lane) % length) / length
+    width = length // n
+    bins = width * (lane % n) + lane // n
+    turn = 2 * np.pi * (np.outer(lane, bins) % length) / length
     both = np.concatenate([np.cos(turn), np.sin(turn)], axis=1).astype(np.float32)
     high = both.astype(jnp.bfloat16)
     low = (both - high.astype(np.float32)).astype(jnp.bfloat16)
     twist = 2 * np.pi * np.outer(np.arange(n), lane) / (n * length)
     scale = 1.0 / np.sqrt(n * length)
-    perm = np.zeros((length, length), np.float32)
-    width = length // n
-    for f in range(n):
-        for e in range(width):
-            perm[f + n * e, f * width + e] = 1.0
     return (
         high, low,
         (np.cos(twist) * scale).astype(np.float32),
         (np.sin(twist) * scale).astype(np.float32),
-        perm,
     )
 
 
 def kernel_shards(echoes, guard_gates, train_gates):
     n = lax.axis_size("pulse")
     length, gates = echoes.shape[1], echoes.shape[2]
-    chunks = CHUNKS if gates % (n * ROWS * CHUNKS) == 0 else 1
+    chunks = CHUNKS
     part = gates // n // chunks
-    smem = pl.BlockSpec(memory_space=pltpu.SMEM)
+    wide = n * part
+    groups = part // ROWS
     vmem = pl.BlockSpec(memory_space=pltpu.VMEM)
     out = jax.ShapeDtypeStruct((length, gates), jnp.float32)
     dma = pltpu.SemaphoreType.DMA
+    operands = (echoes, *(jnp.asarray(t) for t in tables(n, length)))
     results = pl.pallas_call(
         functools.partial(kernel, n, chunks),
         out_shape=(out, out),
-        in_specs=[smem, smem] + [pl.BlockSpec(memory_space=pl.ANY)] * 6,
+        in_specs=[pl.BlockSpec(memory_space=pl.ANY)] * len(operands),
         out_specs=(vmem, vmem),
         scratch_shapes=[
-            pltpu.VMEM((n, chunks, 2, part, length), jnp.float32),
+            pltpu.VMEM((chunks, n, 2, part, length), jnp.float32),
             pltpu.VMEM((chunks, n, 2, part, length), jnp.float32),
             pltpu.VMEM((2, n, part, length), jnp.float32),
-            pltpu.VMEM((n, chunks, part, length), jnp.float32),
-            pltpu.VMEM((n, chunks, part, length), jnp.float32),
-            pltpu.VMEM((length + 2 * ROWS, gates), jnp.float32),
-            pltpu.VMEM((4, ROWS, gates), jnp.float32),
+            pltpu.VMEM((chunks, n, part, length), jnp.float32),
+            pltpu.VMEM((chunks, n, part, length), jnp.float32),
+            pltpu.VMEM((chunks, n, groups, LANES), jnp.float32),
+            pltpu.VMEM((chunks, n, groups, LANES), jnp.float32),
+            pltpu.VMEM((length, length), jnp.bfloat16),
             pltpu.VMEM(echoes.shape, jnp.float32),
             pltpu.VMEM((length, 2 * length), jnp.bfloat16),
             pltpu.VMEM((length, 2 * length), jnp.bfloat16),
             pltpu.VMEM((n, length), jnp.float32),
             pltpu.VMEM((n, length), jnp.float32),
-            pltpu.VMEM((length, length), jnp.float32),
-            dma((chunks, n)), dma((chunks, n)), dma((chunks, n)), dma((chunks, n)),
-            dma((2,)), dma((2,)), dma((7,)),
+            *[dma((chunks, n))] * 6,
+            dma((2 * chunks + 4,)),
+            pltpu.SemaphoreType.REGULAR((n,)),
         ],
         compiler_params=pltpu.CompilerParams(
-            collective_id=0, has_side_effects=True, vmem_limit_bytes=20 * 2**20
+            collective_id=0, has_side_effects=True, vmem_limit_bytes=24 * 2**20
         ),
-    )(guard_gates, train_gates, *(pltpu.with_memory_space_constraint(t, pltpu.HBM) for t in (echoes, *(jnp.asarray(t) for t in tables(n, length)))))
+        cost_estimate=pl.CostEstimate(
+            flops=KERNEL_FLOPS, bytes_accessed=2 * 4 * length * gates, transcendentals=0
+        ),
+    )(*(pltpu.with_memory_space_constraint(t, pltpu.HBM) for t in operands))
     return pl.pallas_call(
         write_out,
         out_shape=(out, out),
-        in_specs=[vmem] * 2,
+        in_specs=[vmem] * 4,
         out_specs=(pl.BlockSpec(memory_space=pl.ANY),) * 2,
-        scratch_shapes=[dma((2,))],
-        compiler_params=pltpu.CompilerParams(vmem_limit_bytes=8 * 2**20),
-    )(*results)
-
-
-def write_out(power_in, stat_in, power_out, stat_out, done):
-    copies = [
-        pltpu.make_async_copy(power_in, power_out, done.at[0]),
-        pltpu.make_async_copy(stat_in, stat_out, done.at[1]),
-    ]
-    for copy in copies:
-        copy.start()
+        scratch_shapes=[pltpu.VMEM((length, gates), jnp.float32), dma((1 + gates // BLOCK,))],
+        compiler_params=pltpu.CompilerParams(vmem_limit_bytes=12 * 2**20),
+    )(guard_gates, train_gates, *results)
+
+
+def write_out(guard_ref, train_ref, power_in, total_in, power_out, stat_out, stat_ref, done):
+    gates = power_in.shape[1]
+    copies = [pltpu.make_async_copy(power_in, power_out, done.at[0])]
+    copies[0].start()
+    guard, train = guard_ref[...].reshape(1, 1), train_ref[...].reshape(1, 1)
+    rows = BLOCK + 2 * LANES
+    taps = lax.broadcasted_iota(jnp.int32, (rows, BLOCK), 0) - LANES
+    taps = jnp.abs(taps - lax.broadcasted_iota(jnp.int32, (rows, BLOCK), 1))
+    inside = (taps > guard) & (taps <= guard + train)
+    band = inside.astype(jnp.float32).astype(jnp.bfloat16)
+    gate = lax.broadcasted_iota(jnp.int32, (1, gates), 1)
+    before = jnp.minimum(jnp.maximum(gate - guard, 0), train)
+    after = jnp.minimum(jnp.maximum(gates - 1 - gate - guard, 0), train)
+    count = (before + after).astype(jnp.float32) + 2.0 * TRAIN_BINS
+    high, low = split(power_in[...])
+    for first in range(0, gates, BLOCK):
+        last = min(first + BLOCK, gates)
+        begin, end = max(0, first - LANES), min(gates, last + LANES)
+        taps = band[begin - first + LANES : end - first + LANES, : last - first]
+        total = bf16_dot(high[:, begin:end], taps) + bf16_dot(low[:, begin:end], taps)
+        scale = count[:, first:last]
+        total = total + total_in[:, first:last] + scale
+        stat_ref[:, first:last] = power_in[:, first:last] * scale / total
+        copies.append(
+            pltpu.make_async_copy(
+                stat_ref.at[:, first:last], stat_out.at[:, first:last], done.at[len(copies)]
+            )
+        )
+        copies[-1].start()
     for copy in copies:
         copy.wait()
 
 
 CHUNKS = 2
+BLOCK = 256
+KERNEL_FLOPS = 10**10
+PLANE = 4
+PLANES = 4
+REACH = 20
 
 
 def shards(echoes, guard_gates, train_gates):
     n = lax.axis_size("pulse")
     length, gates = echoes.shape[1], echoes.shape[2]
-    fits = length % LANES == 0 and length % n == 0 and n > 2 and gates % (n * ROWS) == 0
-    fits = fits and n & (n - 1) == 0 and length & (length - 1) == 0 and LANES % (length // n) == 0
+    fits = length % LANES == 0 and length % n == 0 and 2 < n <= LANES
+    fits = fits and gates % (n * ROWS * CHUNKS) == 0 and gates % (LANES * CHUNKS) == 0
+    fits = fits and n & (n - 1) == 0 and length & (length - 1) == 0 and REACH <= LANES
     if fits and GUARD_BINS + TRAIN_BINS <= ROWS:
         return kernel_shards(echoes, guard_gates, train_gates)
     return generic_shards(echoes, guard_gates, train_gates)

time: 67 us -> 64.7 us (0.966)
  Pallas kernels: 65 us -> 62.6 us
    pallas_call x1, Pallas kernels: 63.8 us -> 61.2 us  [kernel_shards(): pl.pallas_call(functools.partial(kernel, n, chunks), out_shape=(out, out)...]
where the time goes in v1:
time: 64.7 us; the launch traced here: 64.5 us
  Pallas kernels  62.6 us (97%)
  between operations  1.93 us (3%)
    pallas_call x1, Pallas kernels, kernel_shards(): pl.pallas_call(functools.partial(kernel, n, chunks), out_shape=(out, out)...  61.2 us
    pallas_call x1, Pallas kernels, kernel_shards(): pl.pallas_call(write_out, out_shape=(out, out), in_specs=[vmem] * 4, out_...  1.45 us

profile of v1, /device:TPU:0, one launch (start us, length us, event | category | flops | bytes accessed | tf_op | source)
XLA Modules:
  0.0 64.5 jit_solution(270618542776541130)
XLA Ops:
  1.9 61.2 %shard_map.86 = (f32[256,768]{1,0:T(8,128)S(1)}, f32[256,768]{1,0:T(8,128)S(1)}) custom-call(f32[2,256,768]{2,1,0:T(8,128)} %x_any.1, bf16[256,512]{1,0:T(8,128)(2,1)} %constant.8.clone.high_any, bf16[256,512]{1,0:T(8,128)(2,1)} %constant.9.clone.low_any, f32[16,256]{1,0:T(8,128)} %constant.10.clone.cos_any, f32[16,256]{1,0:T(8,128)} %constant.11.clone.sin_any), custom_call_target="tpu_custom_call" | custom-call | flops 10000000000 | bytes 1572864 | tf_op jit(solution)/shard_map/pallas_call | solution.py:415
  63.1 1.4 %shard_map.87 = (f32[256,768]{1,0:T(8,128)}, f32[256,768]{1,0:T(8,128)}) custom-call(s32[1]{0:T(128)S(6)} %copy.9.guard_ref, s32[1]{0:T(128)S(6)} %copy.10.train_ref, f32[256,768]{1,0:T(8,128)S(1)} %get-tuple-element.4.power_in, f32[256,768]{1,0:T(8,128)S(1)} %get-tuple-element.5.total_in), custom_call_target="tpu_custom_call" | custom-call | tf_op jit(solution)/shard_map/pallas_call | solution.py:445

commit v2 on v1

--- a/solution.py
+++ b/solution.py
@@ -189,18 +189,21 @@
 def peer_orders(n):
     ascending = list(range(1, n))
     if n != PLANES * PLANE:
-        return ascending, ascending
-    hops = [[plane * PLANE + own for own in range(PLANE)] for plane in range(PLANES)]
-    own = hops[0][1:]
-    return hops[1] + hops[2] + hops[3] + own, hops[3] + hops[2] + hops[1] + own
+        return ((ascending, ascending),) * 2
+    near, far, across = ([hop * PLANE + own for own in range(PLANE)] for hop in range(1, PLANES))
+    own = ascending[: PLANE - 1]
+    there = (far + across + near + own, far + across + near + own)
+    back = (across + near + far + own, far + across + own + near)
+    return there, back
 
 
 def kernel(
-    n, chunks, x_any, high_any, low_any, cos_any, sin_any,
-    power_ref, total_ref,
-    sent, got, mixed, cells, landed, halo_out, halo_in, near_ref,
-    x_ref, table_high, table_low, twist_cos, twist_sin,
-    send_one, recv_one, send_two, recv_two, send_halo, recv_halo, load, ready,
+    n, chunks, x_any, guard_any, train_any, high_any, low_any, cos_any, sin_any,
+    power_ref, total_ref, scale_ref, band_ref, near_ref,
+    sent, got, mixed, cells, landed, halo_out, halo_in, edges,
+    x_ref, guard_ref, train_ref, table_high, table_low, twist_cos, twist_sin,
+    send_one, recv_one, send_two, recv_two, send_halo, recv_halo, send_edge, recv_edge,
+    load, ready,
 ):
     me = lax.axis_index("pulse")
     length, gates = x_ref.shape[1], x_ref.shape[2]
@@ -209,22 +212,22 @@
     halves = length // LANES
     groups = part // ROWS
     barrier = pltpu.get_barrier_semaphore()
+    tiles = wide // LANES
+    loads = []
+    for t in range(chunks * tiles):
+        lanes = slice(t * LANES, (t + 1) * LANES)
+        loads.append((x_any.at[:, :, lanes], x_ref.at[:, :, lanes]))
+    loads += [
+        (guard_any, guard_ref), (train_any, train_ref), (cos_any, twist_cos),
+        (sin_any, twist_sin), (high_any, table_high), (low_any, table_low),
+    ]
+    loads = [pltpu.make_async_copy(*pair, load.at[i]) for i, pair in enumerate(loads)]
+    for copy in loads:
+        copy.start()
     for k in range(1, n):
         @pl.when(me + k < n)
         def _():
             pl.semaphore_signal(barrier, inc=1, device_id={"pulse": lax.rem(me + k, n)})
-    loads = []
-    for c in range(chunks):
-        for p in range(2):
-            lanes = slice(c * wide, (c + 1) * wide)
-            loads.append((x_any.at[p, :, lanes], x_ref.at[p, :, lanes]))
-    loads += [
-        (cos_any, twist_cos), (sin_any, twist_sin), (high_any, table_high), (low_any, table_low),
-    ]
-    loads = [pltpu.make_async_copy(*pair, load.at[i]) for i, pair in enumerate(loads)]
-    for copy in loads:
-        copy.start()
-
     @pl.when(me > 0)
     def _():
         pl.semaphore_wait(barrier, me)
@@ -236,25 +239,24 @@
                 ready.at[me], inc=1, device_id={"pulse": lax.rem(me + n - k, n)}
             )
 
-    def fill(c):
+    def fill(t):
+        loads[t].wait()
+        c, first = t // tiles, t % tiles * LANES
         for p in range(2):
-            loads[2 * c + p].wait()
-            block = x_ref[p, :, c * wide : (c + 1) * wide].T
-            sent[c, :, p] = block.reshape(n, part, length)
+            block = x_ref[p, :, t * LANES : (t + 1) * LANES].T
+            for d in range(first // part, -(-(first + LANES) // part)):
+                begin, end = max(first, d * part), min(first + LANES, (d + 1) * part)
+                sent[c, d, p, begin - d * part : end - d * part] = block[begin - first : end - first]
 
     inner = inner_flag(me, n)
-    outer_order, inner_order = peer_orders(n)
-    peers = []
-    for a, b in zip(outer_order, inner_order):
-        if a == b:
-            peers.append((a, partner(me, a)))
-        else:
-            peers.append(
-                (
-                    a + inner * (b - a),
-                    (1 - inner) * partner(me, a) + inner * partner(me, b),
-                )
-            )
+    peers, back = (
+        [
+            (a + inner * (b - a), (1 - inner) * partner(me, a) + inner * partner(me, b))
+            if a != b else (a, partner(me, a))
+            for a, b in zip(*orders)
+        ]
+        for orders in peer_orders(n)
+    )
 
     def first_copy(c, o, peer):
         return pltpu.make_async_remote_copy(
@@ -270,28 +272,53 @@
             device_id={"pulse": peer},
         )
 
-    def halo_copy(c, o, peer):
+    def halo_copy(o, peer):
         return pltpu.make_async_remote_copy(
-            src_ref=halo_out.at[c, peer], dst_ref=halo_in.at[c, me],
-            send_sem=send_halo.at[c, o], recv_sem=recv_halo.at[c, o],
+            src_ref=halo_out.at[peer], dst_ref=halo_in.at[me],
+            send_sem=send_halo.at[o], recv_sem=recv_halo.at[o],
             device_id={"pulse": peer},
         )
 
-    fill(0)
+    plane, place = lax.div(me, PLANE), lax.rem(me, PLANE)
+    below = 0
+    for t in range(tiles):
+        fill(t)
+        covered = (t + 1) * LANES // (part * PLANE)
+        for low_plane in range(below, covered):
+            @pl.when(plane > low_plane)
+            def _():
+                for own in range(PLANE):
+                    o = partner(plane, low_plane) * PLANE + own
+                    first_copy(0, o, low_plane * PLANE + partner(place, own)).start()
+
+        below = covered
     for o, peer in peers:
-        @pl.when(peer > me)
+        @pl.when(lax.div(peer, PLANE) >= plane)
         def _():
-            pl.semaphore_wait(ready.at[peer], 1)
-
-        first_copy(0, o, peer).start()
+            @pl.when(peer > me)
+            def _():
+                pl.semaphore_wait(ready.at[peer], 1)
+
+            first_copy(0, o, peer).start()
+
     for c in range(1, chunks):
-        fill(c)
+        for t in range(c * tiles, (c + 1) * tiles):
+            fill(t)
         for o, peer in peers:
             first_copy(c, o, peer).start()
     for c in range(chunks):
         got[c, me] = sent[c, me]
-    for copy in loads[2 * chunks :]:
+    for copy in loads[chunks * tiles :]:
         copy.wait()
+    guard, train = guard_ref[0], train_ref[0]
+    taps = lax.broadcasted_iota(jnp.int32, band_ref.shape, 0) - LANES
+    taps = jnp.abs(taps - lax.broadcasted_iota(jnp.int32, band_ref.shape, 1))
+    inside = (taps > guard) & (taps <= guard + train)
+    band_ref[...] = inside.astype(jnp.float32).astype(jnp.bfloat16)
+    gate = lax.broadcasted_iota(jnp.int32, scale_ref.shape, 1)
+    before = jnp.minimum(jnp.maximum(gate - guard, 0), train)
+    after = jnp.minimum(jnp.maximum(gates - 1 - gate - guard, 0), train)
+    scale_ref[...] = (before + after).astype(jnp.float32) + 2.0 * TRAIN_BINS
     bins = lax.broadcasted_iota(jnp.int32, (length, length), 0)
     bins = jnp.abs(bins - lax.broadcasted_iota(jnp.int32, (length, length), 1))
     inside = (bins > GUARD_BINS) & (bins <= GUARD_BINS + TRAIN_BINS)
@@ -324,64 +351,117 @@
             [power[f, :, h * LANES : (h + 1) * LANES] for h in range(halves)] for f in range(n)
         ]
         rows = swap_digits(rows, 1)
-        lane = lax.broadcasted_iota(jnp.int32, (part, LANES), 1)
         for d in range(n):
             for h in range(halves):
                 cells[c, d, :, h * LANES : (h + 1) * LANES] = rows[d][h]
+        if c < chunks - 1:
+            return
+        lane = lax.broadcasted_iota(jnp.int32, (part, LANES), 1)
         for d in range(n):
             ends = jnp.where(
                 lane >= LANES - ROWS, rows[(d + n - 1) % n][halves - 1],
                 jnp.where(lane < ROWS, rows[(d + 1) % n][0], 0.0),
             )
             ends = pltpu.roll(ends, ROWS, 1, stride=2 * ROWS, stride_axis=0)
-            halo_out[c, d] = jnp.sum(ends.reshape(groups, ROWS, LANES), axis=1)
+            halo_out[d] = jnp.sum(ends.reshape(groups, ROWS, LANES), axis=1)
 
     for c in range(chunks):
         for o, peer in peers:
             first_copy(c, o, peer).wait_recv()
         spectra(c)
-        for o, peer in peers:
-            halo_copy(c, o, peer).start()
+        for o, peer in back:
+            if c == chunks - 1:
+                halo_copy(o, peer).start()
             second_copy(c, o, peer).start()
         landed[c, me] = cells[c, me]
-        halo_in[c, me] = halo_out[c, me]
-
-    row = lax.broadcasted_iota(jnp.int32, (wide, LANES), 0)
-    lane = lax.broadcasted_iota(jnp.int32, (wide, LANES), 1)
-    mine = lane // (2 * ROWS) == row % ROWS
-    slot = lax.broadcasted_iota(jnp.int32, (2 * ROWS, LANES), 0)
-    lane = lax.broadcasted_iota(jnp.int32, (2 * ROWS, LANES), 1)
-    fold = (lane % (2 * ROWS) == slot).astype(jnp.float32).astype(jnp.bfloat16)
+    halo_in[me] = halo_out[me]
+
+    def edge_copies(c):
+        ends = ((length - ROWS, 0, 1), (0, 1, n - 1))
+        return [
+            pltpu.make_async_remote_copy(
+                src_ref=power_ref.at[row : row + ROWS, c * wide : (c + 1) * wide],
+                dst_ref=edges.at[c, side],
+                send_sem=send_edge.at[c, side], recv_sem=recv_edge.at[c, side],
+                device_id={"pulse": lax.rem(me + hop, n)},
+            )
+            for row, side, hop in ends
+        ]
+
+    def arrive(c):
+        for o, peer in peers:
+            second_copy(c, o, peer).wait_recv()
+        power_ref[:, c * wide : (c + 1) * wide] = landed[c].reshape(wide, length).T
+
     rest = jnp.zeros((ROWS, wide), jnp.float32)
 
-    for c in range(chunks):
-        for o, peer in peers:
-            halo_copy(c, o, peer).wait_recv()
-            second_copy(c, o, peer).wait_recv()
-        columns = slice(c * wide, (c + 1) * wide)
-        powers = landed[c].reshape(wide, length).T
-        power_ref[:, columns] = powers
-        high, low = split(powers)
-        total = bf16_dot(near_ref[...], high) + bf16_dot(near_ref[...], low)
-        packed = halo_in[c].reshape(n * groups, 1, LANES)
-        packed = jnp.broadcast_to(packed, (n * groups, ROWS, LANES)).reshape(wide, LANES)
-        high, low = split(jnp.where(mine, packed, 0.0))
-        last_dims = (((1,), (1,)), ((), ()))
-        halos = bf16_dot(fold, high, last_dims) + bf16_dot(fold, low, last_dims)
-        head = jnp.concatenate([halos[:ROWS], rest])
-        tail = jnp.concatenate([rest, halos[ROWS:]])
-        top, bottom = total[:ROWS], total[length - ROWS :]
+    def add_edges(columns, before, after):
+        head, tail = jnp.concatenate([before, rest]), jnp.concatenate([rest, after])
+        top, bottom = total_ref[:ROWS, columns], total_ref[length - ROWS :, columns]
         for d in range(GUARD_BINS + 1, GUARD_BINS + TRAIN_BINS + 1):
             top = top + head[ROWS - d : 2 * ROWS - d]
             bottom = bottom + tail[d : d + ROWS]
         total_ref[:ROWS, columns] = top
-        total_ref[ROWS : length - ROWS, columns] = total[ROWS : length - ROWS]
         total_ref[length - ROWS :, columns] = bottom
+
+    final = gates - wide
+    for c in range(chunks - 1):
+        arrive(c)
+        for copy in edge_copies(c):
+            copy.start()
+    total_ref[:, :final] = scale_ref[:1, :final] + near_sum(near_ref, power_ref[:, :final])
+    total_ref[:, final:] = jnp.broadcast_to(scale_ref[:1, final:], (length, wide))
+    for first in range(0, gates, BLOCK):
+        last, begin = min(first + BLOCK, gates), max(0, first - LANES)
+        end = min(final, last + LANES)
+        if begin < end:
+            total_ref[:, first:last] += band_sum(band_ref, power_ref, first, last, begin, end)
+    for c in range(chunks - 1):
+        for copy in edge_copies(c):
+            copy.wait_recv()
+        add_edges(slice(c * wide, (c + 1) * wide), edges[c, 0], edges[c, 1])
+    for first in range(0, gates, BLOCK):
+        if complete(first, gates, final):
+            own = slice(first, min(first + BLOCK, gates))
+            total_ref[:, own] = power_ref[:, own] * scale_ref[:1, own] / total_ref[:, own]
+    for o, peer in peers:
+        halo_copy(o, peer).wait_recv()
+    row = lax.broadcasted_iota(jnp.int32, (wide, LANES), 0)
+    lane = lax.broadcasted_iota(jnp.int32, (wide, LANES), 1)
+    packed = halo_in[...].reshape(n * groups, 1, LANES)
+    packed = jnp.broadcast_to(packed, (n * groups, ROWS, LANES)).reshape(wide, LANES)
+    high, low = split(jnp.where(lane // (2 * ROWS) == row % ROWS, packed, 0.0))
+    slot = lax.broadcasted_iota(jnp.int32, (2 * ROWS, LANES), 0)
+    lane = lax.broadcasted_iota(jnp.int32, (2 * ROWS, LANES), 1)
+    fold = (lane % (2 * ROWS) == slot).astype(jnp.float32).astype(jnp.bfloat16)
+    last_dims = (((1,), (1,)), ((), ()))
+    halos = bf16_dot(fold, high, last_dims) + bf16_dot(fold, low, last_dims)
+    add_edges(slice(final, gates), halos[:ROWS], halos[ROWS:])
+    arrive(chunks - 1)
+    for c in range(chunks - 1):
+        for copy in edge_copies(c):
+            copy.wait_send()
+    for o, peer in peers:
+        halo_copy(o, peer).wait_send()
     for c in range(chunks):
         for o, peer in peers:
             first_copy(c, o, peer).wait_send()
-            halo_copy(c, o, peer).wait_send()
             second_copy(c, o, peer).wait_send()
+
+
+def complete(first, gates, final):
+    return min(gates, first + BLOCK + LANES) <= final
+
+
+def near_sum(near_ref, powers):
+    high, low = split(powers)
+    return bf16_dot(near_ref[...], high) + bf16_dot(near_ref[...], low)
+
+
+def band_sum(band_ref, power_ref, first, last, begin, end):
+    high, low = split(power_ref[:, begin:end])
+    band = band_ref[begin - first + LANES : end - first + LANES, : last - first]
+    return bf16_dot(high, band) + bf16_dot(low, band)
 
 
 def tables(n, length):
@@ -411,28 +491,38 @@
     vmem = pl.BlockSpec(memory_space=pltpu.VMEM)
     out = jax.ShapeDtypeStruct((length, gates), jnp.float32)
     dma = pltpu.SemaphoreType.DMA
-    operands = (echoes, *(jnp.asarray(t) for t in tables(n, length)))
+    constants = tuple(jnp.asarray(t) for t in tables(n, length))
+    echoes, *constants = (
+        pltpu.with_memory_space_constraint(t, pltpu.HBM) for t in (echoes, *constants)
+    )
+    operands = (echoes, guard_gates, train_gates, *constants)
     results = pl.pallas_call(
         functools.partial(kernel, n, chunks),
-        out_shape=(out, out),
+        out_shape=(
+            out, out, jax.ShapeDtypeStruct((ROWS, gates), jnp.float32),
+            jax.ShapeDtypeStruct((BLOCK + 2 * LANES, BLOCK), jnp.bfloat16),
+            jax.ShapeDtypeStruct((length, length), jnp.bfloat16),
+        ),
         in_specs=[pl.BlockSpec(memory_space=pl.ANY)] * len(operands),
-        out_specs=(vmem, vmem),
+        out_specs=(vmem,) * 5,
         scratch_shapes=[
             pltpu.VMEM((chunks, n, 2, part, length), jnp.float32),
             pltpu.VMEM((chunks, n, 2, part, length), jnp.float32),
             pltpu.VMEM((2, n, part, length), jnp.float32),
             pltpu.VMEM((chunks, n, part, length), jnp.float32),
             pltpu.VMEM((chunks, n, part, length), jnp.float32),
-            pltpu.VMEM((chunks, n, groups, LANES), jnp.float32),
-            pltpu.VMEM((chunks, n, groups, LANES), jnp.float32),
-            pltpu.VMEM((length, length), jnp.bfloat16),
+            pltpu.VMEM((n, groups, LANES), jnp.float32),
+            pltpu.VMEM((n, groups, LANES), jnp.float32),
+            pltpu.VMEM((chunks - 1, 2, ROWS, wide), jnp.float32),
             pltpu.VMEM(echoes.shape, jnp.float32),
+            pltpu.SMEM((1,), jnp.int32),
+            pltpu.SMEM((1,), jnp.int32),
             pltpu.VMEM((length, 2 * length), jnp.bfloat16),
             pltpu.VMEM((length, 2 * length), jnp.bfloat16),
             pltpu.VMEM((n, length), jnp.float32),
             pltpu.VMEM((n, length), jnp.float32),
-            *[dma((chunks, n))] * 6,
-            dma((2 * chunks + 4,)),
+            *[dma((chunks, n))] * 4, dma((n,)), dma((n,)),
+            dma((chunks - 1, 2)), dma((chunks - 1, 2)), dma((gates // LANES + 6,)),
             pltpu.SemaphoreType.REGULAR((n,)),
         ],
         compiler_params=pltpu.CompilerParams(
@@ -441,46 +531,46 @@
         cost_estimate=pl.CostEstimate(
             flops=KERNEL_FLOPS, bytes_accessed=2 * 4 * length * gates, transcendentals=0
         ),
-    )(*(pltpu.with_memory_space_constraint(t, pltpu.HBM) for t in operands))
+    )(*operands)
     return pl.pallas_call(
-        write_out,
+        functools.partial(write_out, gates - wide),
         out_shape=(out, out),
-        in_specs=[vmem] * 4,
+        in_specs=[vmem] * 5,
         out_specs=(pl.BlockSpec(memory_space=pl.ANY),) * 2,
         scratch_shapes=[pltpu.VMEM((length, gates), jnp.float32), dma((1 + gates // BLOCK,))],
         compiler_params=pltpu.CompilerParams(vmem_limit_bytes=12 * 2**20),
-    )(guard_gates, train_gates, *results)
-
-
-def write_out(guard_ref, train_ref, power_in, total_in, power_out, stat_out, stat_ref, done):
-    gates = power_in.shape[1]
-    copies = [pltpu.make_async_copy(power_in, power_out, done.at[0])]
-    copies[0].start()
-    guard, train = guard_ref[...].reshape(1, 1), train_ref[...].reshape(1, 1)
-    rows = BLOCK + 2 * LANES
-    taps = lax.broadcasted_iota(jnp.int32, (rows, BLOCK), 0) - LANES
-    taps = jnp.abs(taps - lax.broadcasted_iota(jnp.int32, (rows, BLOCK), 1))
-    inside = (taps > guard) & (taps <= guard + train)
-    band = inside.astype(jnp.float32).astype(jnp.bfloat16)
-    gate = lax.broadcasted_iota(jnp.int32, (1, gates), 1)
-    before = jnp.minimum(jnp.maximum(gate - guard, 0), train)
-    after = jnp.minimum(jnp.maximum(gates - 1 - gate - guard, 0), train)
-    count = (before + after).astype(jnp.float32) + 2.0 * TRAIN_BINS
-    high, low = split(power_in[...])
+    )(*results)
+
+
+def write_out(
+    final, power_ref, total_ref, scale_ref, band_ref, near_ref, power_out, stat_out, stat_ref, done
+):
+    gates = power_ref.shape[1]
+    copies = []
+
+    def put(source, target):
+        copies.append(pltpu.make_async_copy(source, target, done.at[len(copies)]))
+        copies[-1].start()
+
+    put(power_ref, power_out)
     for first in range(0, gates, BLOCK):
+        own = slice(first, min(first + BLOCK, gates))
+        if complete(first, gates, final):
+            put(total_ref.at[:, own], stat_out.at[:, own])
+    for first in range(0, gates, BLOCK):
+        if complete(first, gates, final):
+            continue
         last = min(first + BLOCK, gates)
-        begin, end = max(0, first - LANES), min(gates, last + LANES)
-        taps = band[begin - first + LANES : end - first + LANES, : last - first]
-        total = bf16_dot(high[:, begin:end], taps) + bf16_dot(low[:, begin:end], taps)
-        scale = count[:, first:last]
-        total = total + total_in[:, first:last] + scale
-        stat_ref[:, first:last] = power_in[:, first:last] * scale / total
-        copies.append(
-            pltpu.make_async_copy(
-                stat_ref.at[:, first:last], stat_out.at[:, first:last], done.at[len(copies)]
-            )
-        )
-        copies[-1].start()
+        begin, end = max(final, first - LANES), min(gates, last + LANES)
+        total = total_ref[:, first:last]
+        total = total + band_sum(band_ref, power_ref, first, last, begin, end)
+        late = max(first, final)
+        near = near_sum(near_ref, power_ref[:, late:last])
+        if late > first:
+            near = jnp.concatenate([jnp.zeros_like(power_ref[:, first:late]), near], axis=1)
+        own = slice(first, last)
+        stat_ref[:, own] = power_ref[:, own] * scale_ref[:1, own] / (total + near)
+        put(stat_ref.at[:, own], stat_out.at[:, own])
     for copy in copies:
         copy.wait()
 

time: 64.7 us -> 62.9 us (0.972)
  Pallas kernels: 62.6 us -> 60.8 us
    pallas_call x2, Pallas kernels: 62.6 us -> 60.8 us  [the longest x1 59.5 us: kernel_shards(): pl.pallas_call(functools.partial(kernel, n, chunks), out_shape=(out, out,...]
where the time goes in v2:
time: 62.9 us; the launch traced here: 62.7 us
  Pallas kernels  60.8 us (97%)
  between operations  1.93 us (3%)
    pallas_call x1, Pallas kernels, kernel_shards(): pl.pallas_call(functools.partial(kernel, n, chunks), out_shape=(out, out,...  59.5 us
    pallas_call x1, Pallas kernels, kernel_shards(): pl.pallas_call(functools.partial(write_out, gates - wide), out_shape=(out...  1.26 us

profile of v2, /device:TPU:0, one launch (start us, length us, event | category | flops | bytes accessed | tf_op | source)
XLA Modules:
  0.0 62.7 jit_solution(12886938997823781841)
XLA Ops:
  1.9 59.5 %shard_map.86 = (f32[256,768]{1,0:T(8,128)S(1)}, f32[256,768]{1,0:T(8,128)S(1)}, f32[8,768]{1,0:T(8,128)S(1)}, bf16[512,256]{1,0:T(8,128)(2,1)S(1)}, bf16[256,256]{1,0:T(8,128)(2,1)S(1)}) custom-call(f32[2,256,768]{2,1,0:T(8,128)} %x_any.1, s32[1]{0:T(128)S(6)} %copy.9.guard_any, s32[1]{0:T(128)S(6)} %copy.10.train_any, ...), custom_call_target="tpu_custom_call" | custom-call | flops 10000000000 | bytes 1572864 | tf_op jit(solution)/shard_map/pallas_call | solution.py:499
  61.5 1.3 %shard_map.87 = (f32[256,768]{1,0:T(8,128)}, f32[256,768]{1,0:T(8,128)}) custom-call(f32[256,768]{1,0:T(8,128)S(1)} %get-tuple-element.7.power_ref, f32[256,768]{1,0:T(8,128)S(1)} %get-tuple-element.8.total_ref, f32[8,768]{1,0:T(8,128)S(1)} %get-tuple-element.9.scale_ref, bf16[512,256]{1,0:T(8,128)(2,1)S(1)} %get-tuple-element.10.band_ref, ...), custom_call_target="tpu_custom_call" | custom-call | tf_op jit(solution)/shard_map/pallas_call | solution.py:535

commit v3 on v2

--- a/solution.py
+++ b/solution.py
@@ -203,7 +203,7 @@
     sent, got, mixed, cells, landed, halo_out, halo_in, edges,
     x_ref, guard_ref, train_ref, table_high, table_low, twist_cos, twist_sin,
     send_one, recv_one, send_two, recv_two, send_halo, recv_halo, send_edge, recv_edge,
-    load, ready,
+    load, row_in, last_in, higher, lower, row_known,
 ):
     me = lax.axis_index("pulse")
     length, gates = x_ref.shape[1], x_ref.shape[2]
@@ -224,20 +224,52 @@
     loads = [pltpu.make_async_copy(*pair, load.at[i]) for i, pair in enumerate(loads)]
     for copy in loads:
         copy.start()
-    for k in range(1, n):
-        @pl.when(me + k < n)
-        def _():
-            pl.semaphore_signal(barrier, inc=1, device_id={"pulse": lax.rem(me + k, n)})
-    @pl.when(me > 0)
-    def _():
-        pl.semaphore_wait(barrier, me)
-
-    for k in range(1, n):
-        @pl.when(me >= k)
-        def _():
-            pl.semaphore_signal(
-                ready.at[me], inc=1, device_id={"pulse": lax.rem(me + n - k, n)}
-            )
+    planes = n // PLANE
+    last_plane = planes - 1
+    plane, place = lax.div(me, PLANE), lax.rem(me, PLANE)
+    row, core = lax.div(place, CORES), lax.rem(place, CORES)
+
+    def chip(target, other):
+        return target * PLANE + (row + other - 2 * other * row) * CORES
+
+    def tell(semaphore, target, other):
+        for k in range(CORES):
+            peer = chip(target, other) + k
+            pl.semaphore_signal(semaphore, inc=1, device_id={"pulse": peer})
+
+    def hear(semaphore):
+        pl.semaphore_wait(semaphore, CORES)
+
+    pl.semaphore_signal(barrier, inc=1, device_id={"pulse": partner(me, 1)})
+
+    @pl.when(plane < last_plane)
+    def _():
+        tell(barrier, plane + 1, 0)
+
+    @pl.when((plane >= 1) & (plane < last_plane))
+    def _():
+        tell(barrier, plane - 1, 0)
+
+    @pl.when(row == 0)
+    def _():
+        tell(barrier, plane, 1)
+
+    beneath = lax.div(plane + last_plane, planes)
+    above = 1 - lax.div(plane + 2, planes) if planes > 2 else 0
+    pl.semaphore_wait(barrier, 1 + CORES * (beneath + above + row))
+
+    @pl.when(row == 1)
+    def _():
+        tell(row_in, plane, 1)
+
+    @pl.when((plane == last_plane) & (plane >= 1))
+    def _():
+        tell(last_in, plane - 1, 0)
+
+    @pl.when((plane >= 1) & (plane + 1 < last_plane))
+    def _():
+        tell(higher.at[2], plane - 1, 0)
+        tell(lower.at[2], plane + 1, 0)
 
     def fill(t):
         loads[t].wait()
@@ -258,10 +290,10 @@
         for orders in peer_orders(n)
     )
 
-    def first_copy(c, o, peer):
+    def first_copy(c, peer, source=me):
         return pltpu.make_async_remote_copy(
-            src_ref=sent.at[c, peer], dst_ref=got.at[c, me],
-            send_sem=send_one.at[c, o], recv_sem=recv_one.at[c, o],
+            src_ref=sent.at[c, peer], dst_ref=got.at[c, source],
+            send_sem=send_one.at[c, peer], recv_sem=recv_one.at[c, source],
             device_id={"pulse": peer},
         )
 
@@ -279,33 +311,89 @@
             device_id={"pulse": peer},
         )
 
-    plane, place = lax.div(me, PLANE), lax.rem(me, PLANE)
-    below = 0
+    def send(target, other):
+        for k in range(CORES):
+            first_copy(0, chip(target, other) + partner(core, k)).start()
+
     for t in range(tiles):
         fill(t)
-        covered = (t + 1) * LANES // (part * PLANE)
-        for low_plane in range(below, covered):
-            @pl.when(plane > low_plane)
+
+    @pl.when(plane + 1 < last_plane)
+    def _():
+        send(plane + 1, 0)
+
+    @pl.when(plane >= 1)
+    def _():
+        send(plane - 1, 0)
+
+    first_copy(0, partner(me, 1)).start()
+
+    @pl.when((plane >= 2) & (plane < last_plane))
+    def _():
+        hear(lower.at[2])
+        send(plane - 2, 0)
+
+    @pl.when(plane == last_plane - 1)
+    def _():
+        hear(last_in)
+
+        @pl.when(plane >= 1)
+        def _():
+            tell(higher.at[2], plane - 1, 0)
+            tell(lower.at[2], plane + 1, 0)
+
+        send(plane + 1, 0)
+
+    @pl.when(row == 0)
+    def _():
+        hear(row_in)
+
+    tell(row_known.at[1], plane, 1)
+    hear(row_known.at[1])
+    for hop in (1, -1):
+        @pl.when((plane + hop >= 0) & (plane + hop <= last_plane))
+        def _():
+            send(plane + hop, 1)
+
+    send(plane, 1)
+    for k in range(2, planes):
+        @pl.when(plane + k <= last_plane)
+        def _():
+            hear(higher.at[k])
+
+        @pl.when((plane >= k) if k > 2 else (plane == last_plane))
+        def _():
+            hear(lower.at[k])
+
+        if k + 1 < planes:
+            @pl.when((plane + k <= last_plane) & (plane >= 1))
             def _():
-                for own in range(PLANE):
-                    o = partner(plane, low_plane) * PLANE + own
-                    first_copy(0, o, low_plane * PLANE + partner(place, own)).start()
-
-        below = covered
-    for o, peer in peers:
-        @pl.when(lax.div(peer, PLANE) >= plane)
+                tell(higher.at[k + 1], plane - 1, 0)
+
+            @pl.when((plane >= k) & (plane < last_plane))
+            def _():
+                tell(lower.at[k + 1], plane + 1, 0)
+
+        @pl.when(plane + k <= last_plane)
         def _():
-            @pl.when(peer > me)
+            send(plane + k, 0)
+
+        @pl.when((plane >= k) if k > 2 else (plane == last_plane))
+        def _():
+            send(plane - k, 0)
+
+        tell(row_known.at[k], plane, 1)
+        hear(row_known.at[k])
+        for hop in (k, -k):
+            @pl.when((plane + hop >= 0) & (plane + hop <= last_plane))
             def _():
-                pl.semaphore_wait(ready.at[peer], 1)
-
-            first_copy(0, o, peer).start()
+                send(plane + hop, 1)
 
     for c in range(1, chunks):
         for t in range(c * tiles, (c + 1) * tiles):
             fill(t)
         for o, peer in peers:
-            first_copy(c, o, peer).start()
+            first_copy(c, peer).start()
     for c in range(chunks):
         got[c, me] = sent[c, me]
     for copy in loads[chunks * tiles :]:
@@ -367,7 +455,7 @@
 
     for c in range(chunks):
         for o, peer in peers:
-            first_copy(c, o, peer).wait_recv()
+            first_copy(c, peer, peer).wait_recv()
         spectra(c)
         for o, peer in back:
             if c == chunks - 1:
@@ -426,11 +514,11 @@
             total_ref[:, own] = power_ref[:, own] * scale_ref[:1, own] / total_ref[:, own]
     for o, peer in peers:
         halo_copy(o, peer).wait_recv()
-    row = lax.broadcasted_iota(jnp.int32, (wide, LANES), 0)
+    gate_row = lax.broadcasted_iota(jnp.int32, (wide, LANES), 0)
     lane = lax.broadcasted_iota(jnp.int32, (wide, LANES), 1)
     packed = halo_in[...].reshape(n * groups, 1, LANES)
     packed = jnp.broadcast_to(packed, (n * groups, ROWS, LANES)).reshape(wide, LANES)
-    high, low = split(jnp.where(lane // (2 * ROWS) == row % ROWS, packed, 0.0))
+    high, low = split(jnp.where(lane // (2 * ROWS) == gate_row % ROWS, packed, 0.0))
     slot = lax.broadcasted_iota(jnp.int32, (2 * ROWS, LANES), 0)
     lane = lax.broadcasted_iota(jnp.int32, (2 * ROWS, LANES), 1)
     fold = (lane % (2 * ROWS) == slot).astype(jnp.float32).astype(jnp.bfloat16)
@@ -445,7 +533,7 @@
         halo_copy(o, peer).wait_send()
     for c in range(chunks):
         for o, peer in peers:
-            first_copy(c, o, peer).wait_send()
+            first_copy(c, peer).wait_send()
             second_copy(c, o, peer).wait_send()
 
 
@@ -523,7 +611,8 @@
             pltpu.VMEM((n, length), jnp.float32),
             *[dma((chunks, n))] * 4, dma((n,)), dma((n,)),
             dma((chunks - 1, 2)), dma((chunks - 1, 2)), dma((gates // LANES + 6,)),
-            pltpu.SemaphoreType.REGULAR((n,)),
+            pltpu.SemaphoreType.REGULAR, pltpu.SemaphoreType.REGULAR,
+            *[pltpu.SemaphoreType.REGULAR((max(3, n // PLANE),))] * 3,
         ],
         compiler_params=pltpu.CompilerParams(
             collective_id=0, has_side_effects=True, vmem_limit_bytes=24 * 2**20
@@ -579,6 +668,7 @@
 BLOCK = 256
 KERNEL_FLOPS = 10**10
 PLANE = 4
+CORES = 2
 PLANES = 4
 REACH = 20
 
@@ -586,7 +676,7 @@
 def shards(echoes, guard_gates, train_gates):
     n = lax.axis_size("pulse")
     length, gates = echoes.shape[1], echoes.shape[2]
-    fits = length % LANES == 0 and length % n == 0 and 2 < n <= LANES
+    fits = length % LANES == 0 and length % n == 0 and n % PLANE == 0 and n <= LANES
     fits = fits and gates % (n * ROWS * CHUNKS) == 0 and gates % (LANES * CHUNKS) == 0
     fits = fits and n & (n - 1) == 0 and length & (length - 1) == 0 and REACH <= LANES
     if fits and GUARD_BINS + TRAIN_BINS <= ROWS:

time: 62.9 us -> 61.8 us (0.983)
  Pallas kernels: 60.8 us -> 59.7 us
    pallas_call x1, Pallas kernels: 59.5 us -> 58.4 us  [kernel_shards(): pl.pallas_call(functools.partial(kernel, n, chunks), out_shape=(out, out,...]
where the time goes in v3:
time: 61.8 us; the launch traced here: 61.6 us
  Pallas kernels  59.7 us (97%)
  between operations  1.93 us (3%)
    pallas_call x1, Pallas kernels, kernel_shards(): pl.pallas_call(functools.partial(kernel, n, chunks), out_shape=(out, out,...  58.4 us
    pallas_call x1, Pallas kernels, kernel_shards(): pl.pallas_call(functools.partial(write_out, gates - wide), out_shape=(out...  1.26 us

profile of v3, /device:TPU:0, one launch (start us, length us, event | category | flops | bytes accessed | tf_op | source)
XLA Modules:
  0.0 61.6 jit_solution(3571712250155944790)
XLA Ops:
  1.9 58.4 %shard_map.86 = (f32[256,768]{1,0:T(8,128)S(1)}, f32[256,768]{1,0:T(8,128)S(1)}, f32[8,768]{1,0:T(8,128)S(1)}, bf16[512,256]{1,0:T(8,128)(2,1)S(1)}, bf16[256,256]{1,0:T(8,128)(2,1)S(1)}) custom-call(f32[2,256,768]{2,1,0:T(8,128)} %x_any.1, s32[1]{0:T(128)S(6)} %copy.9.guard_any, s32[1]{0:T(128)S(6)} %copy.10.train_any, ...), custom_call_target="tpu_custom_call" | custom-call | flops 10000000000 | bytes 1572864 | tf_op jit(solution)/shard_map/pallas_call | solution.py:587
  60.3 1.3 %shard_map.87 = (f32[256,768]{1,0:T(8,128)}, f32[256,768]{1,0:T(8,128)}) custom-call(f32[256,768]{1,0:T(8,128)S(1)} %get-tuple-element.7.power_ref, f32[256,768]{1,0:T(8,128)S(1)} %get-tuple-element.8.total_ref, f32[8,768]{1,0:T(8,128)S(1)} %get-tuple-element.9.scale_ref, bf16[512,256]{1,0:T(8,128)(2,1)S(1)} %get-tuple-element.10.band_ref, ...), custom_call_target="tpu_custom_call" | custom-call | tf_op jit(solution)/shard_map/pallas_call | solution.py:624

commit v4 on v3

--- a/solution.py
+++ b/solution.py
@@ -192,8 +192,9 @@
         return ((ascending, ascending),) * 2
     near, far, across = ([hop * PLANE + own for own in range(PLANE)] for hop in range(1, PLANES))
     own = ascending[: PLANE - 1]
-    there = (far + across + near + own, far + across + near + own)
-    back = (across + near + far + own, far + across + own + near)
+    there = (near + far + across + own, far + across + near + own)
+    near, far, across = near[::-1], far[::-1], across[::-1]
+    back = (across + near + far + own, near + far + across + own)
     return there, back
 
 
@@ -297,18 +298,34 @@
             device_id={"pulse": peer},
         )
 
-    def second_copy(c, o, peer):
+    def second_copy(c, peer, source=me):
+        rows = pl.ds(pl.multiple_of(source * part, ROWS), part)
         return pltpu.make_async_remote_copy(
-            src_ref=cells.at[c, peer], dst_ref=landed.at[c, me],
-            send_sem=send_two.at[c, o], recv_sem=recv_two.at[c, o],
+            src_ref=cells.at[c, peer], dst_ref=landed.at[c, rows],
+            send_sem=send_two.at[c], recv_sem=recv_two.at[c, source],
             device_id={"pulse": peer},
         )
 
-    def halo_copy(o, peer):
+    def halo_copy(peer):
         return pltpu.make_async_remote_copy(
             src_ref=halo_out.at[peer], dst_ref=halo_in.at[me],
-            send_sem=send_halo.at[o], recv_sem=recv_halo.at[o],
+            send_sem=send_halo, recv_sem=recv_halo,
             device_id={"pulse": peer},
+        )
+
+    def all_halos():
+        others = pl.ds(0, n - 1)
+        return pltpu.make_async_remote_copy(
+            src_ref=halo_out.at[others], dst_ref=halo_in.at[others],
+            send_sem=send_halo, recv_sem=recv_halo, device_id={"pulse": partner(me, 1)},
+        )
+
+    def all_sent(c):
+        others = cells.at[c, pl.ds(0, n - 1)]
+        return pltpu.make_async_remote_copy(
+            src_ref=others, dst_ref=others,
+            send_sem=send_two.at[c], recv_sem=recv_two.at[c, 0],
+            device_id={"pulse": partner(me, 1)},
         )
 
     def send(target, other):
@@ -459,9 +476,9 @@
         spectra(c)
         for o, peer in back:
             if c == chunks - 1:
-                halo_copy(o, peer).start()
-            second_copy(c, o, peer).start()
-        landed[c, me] = cells[c, me]
+                halo_copy(peer).start()
+            second_copy(c, peer).start()
+        landed[c, pl.ds(pl.multiple_of(me * part, ROWS), part)] = cells[c, me]
     halo_in[me] = halo_out[me]
 
     def edge_copies(c):
@@ -476,10 +493,24 @@
             for row, side, hop in ends
         ]
 
+    upper = lax.div(2 * me, n)
+
     def arrive(c):
-        for o, peer in peers:
-            second_copy(c, o, peer).wait_recv()
-        power_ref[:, c * wide : (c + 1) * wide] = landed[c].reshape(wide, length).T
+        below = 0
+        for k in range(tiles):
+            covered = -(-(k + 1) * LANES // part)
+            for d in range(below, covered):
+                peer = d + upper * (n - 1 - 2 * d)
+
+                @pl.when(peer != me)
+                def _():
+                    second_copy(c, peer, peer).wait_recv()
+
+            below = covered
+            first = (k + upper * (tiles - 1 - 2 * k)) * LANES
+            rows = pl.ds(pl.multiple_of(first, LANES), LANES)
+            columns = pl.ds(pl.multiple_of(c * wide + first, LANES), LANES)
+            power_ref[:, columns] = landed[c, rows].T
 
     rest = jnp.zeros((ROWS, wide), jnp.float32)
 
@@ -512,8 +543,15 @@
         if complete(first, gates, final):
             own = slice(first, min(first + BLOCK, gates))
             total_ref[:, own] = power_ref[:, own] * scale_ref[:1, own] / total_ref[:, own]
-    for o, peer in peers:
-        halo_copy(o, peer).wait_recv()
+    for c in range(chunks):
+        for o, peer in peers:
+            first_copy(c, peer).wait_send()
+        if c < chunks - 1:
+            all_sent(c).wait_send()
+    for c in range(chunks - 1):
+        for copy in edge_copies(c):
+            copy.wait_send()
+    all_halos().wait_recv()
     gate_row = lax.broadcasted_iota(jnp.int32, (wide, LANES), 0)
     lane = lax.broadcasted_iota(jnp.int32, (wide, LANES), 1)
     packed = halo_in[...].reshape(n * groups, 1, LANES)
@@ -526,15 +564,8 @@
     halos = bf16_dot(fold, high, last_dims) + bf16_dot(fold, low, last_dims)
     add_edges(slice(final, gates), halos[:ROWS], halos[ROWS:])
     arrive(chunks - 1)
-    for c in range(chunks - 1):
-        for copy in edge_copies(c):
-            copy.wait_send()
-    for o, peer in peers:
-        halo_copy(o, peer).wait_send()
-    for c in range(chunks):
-        for o, peer in peers:
-            first_copy(c, peer).wait_send()
-            second_copy(c, o, peer).wait_send()
+    all_halos().wait_send()
+    all_sent(chunks - 1).wait_send()
 
 
 def complete(first, gates, final):
@@ -598,7 +629,7 @@
             pltpu.VMEM((chunks, n, 2, part, length), jnp.float32),
             pltpu.VMEM((2, n, part, length), jnp.float32),
             pltpu.VMEM((chunks, n, part, length), jnp.float32),
-            pltpu.VMEM((chunks, n, part, length), jnp.float32),
+            pltpu.VMEM((chunks, wide, length), jnp.float32),
             pltpu.VMEM((n, groups, LANES), jnp.float32),
             pltpu.VMEM((n, groups, LANES), jnp.float32),
             pltpu.VMEM((chunks - 1, 2, ROWS, wide), jnp.float32),
@@ -609,7 +640,7 @@
             pltpu.VMEM((length, 2 * length), jnp.bfloat16),
             pltpu.VMEM((n, length), jnp.float32),
             pltpu.VMEM((n, length), jnp.float32),
-            *[dma((chunks, n))] * 4, dma((n,)), dma((n,)),
+            *[dma((chunks, n))] * 2, dma((chunks,)), dma((chunks, n)), dma, dma,
             dma((chunks - 1, 2)), dma((chunks - 1, 2)), dma((gates // LANES + 6,)),
             pltpu.SemaphoreType.REGULAR, pltpu.SemaphoreType.REGULAR,
             *[pltpu.SemaphoreType.REGULAR((max(3, n // PLANE),))] * 3,

time: 61.8 us -> 60.6 us (0.981)
  Pallas kernels: 59.7 us -> 58.2 us
    pallas_call x1, Pallas kernels: 58.4 us -> 57 us  [kernel_shards(): pl.pallas_call(functools.partial(kernel, n, chunks), out_shape=(out, out,...]
where the time goes in v4:
time: 60.6 us; the launch traced here: 60.2 us
  Pallas kernels  58.2 us (96%)
  between operations  1.93 us (3%)
    pallas_call x1, Pallas kernels, kernel_shards(): pl.pallas_call(functools.partial(kernel, n, chunks), out_shape=(out, out,...  57 us
    pallas_call x1, Pallas kernels, kernel_shards(): pl.pallas_call(functools.partial(write_out, gates - wide), out_shape=(out...  1.26 us

profile of v4, /device:TPU:0, one launch (start us, length us, event | category | flops | bytes accessed | tf_op | source)
XLA Modules:
  0.0 60.2 jit_solution(6538545585486236289)
XLA Ops:
  1.9 57.0 %shard_map.86 = (f32[256,768]{1,0:T(8,128)S(1)}, f32[256,768]{1,0:T(8,128)S(1)}, f32[8,768]{1,0:T(8,128)S(1)}, bf16[512,256]{1,0:T(8,128)(2,1)S(1)}, bf16[256,256]{1,0:T(8,128)(2,1)S(1)}) custom-call(f32[2,256,768]{2,1,0:T(8,128)} %x_any.1, s32[1]{0:T(128)S(6)} %copy.9.guard_any, s32[1]{0:T(128)S(6)} %copy.10.train_any, ...), custom_call_target="tpu_custom_call" | custom-call | flops 10000000000 | bytes 1572864 | tf_op jit(solution)/shard_map/pallas_call | solution.py:618
  58.9 1.3 %shard_map.87 = (f32[256,768]{1,0:T(8,128)}, f32[256,768]{1,0:T(8,128)}) custom-call(f32[256,768]{1,0:T(8,128)S(1)} %get-tuple-element.7.power_ref, f32[256,768]{1,0:T(8,128)S(1)} %get-tuple-element.8.total_ref, f32[8,768]{1,0:T(8,128)S(1)} %get-tuple-element.9.scale_ref, bf16[512,256]{1,0:T(8,128)(2,1)S(1)} %get-tuple-element.10.band_ref, ...), custom_call_target="tpu_custom_call" | custom-call | tf_op jit(solution)/shard_map/pallas_call | solution.py:655

commit v5 on v4

--- a/solution.py
+++ b/solution.py
@@ -255,23 +255,6 @@
     def _():
         tell(barrier, plane, 1)
 
-    beneath = lax.div(plane + last_plane, planes)
-    above = 1 - lax.div(plane + 2, planes) if planes > 2 else 0
-    pl.semaphore_wait(barrier, 1 + CORES * (beneath + above + row))
-
-    @pl.when(row == 1)
-    def _():
-        tell(row_in, plane, 1)
-
-    @pl.when((plane == last_plane) & (plane >= 1))
-    def _():
-        tell(last_in, plane - 1, 0)
-
-    @pl.when((plane >= 1) & (plane + 1 < last_plane))
-    def _():
-        tell(higher.at[2], plane - 1, 0)
-        tell(lower.at[2], plane + 1, 0)
-
     def fill(t):
         loads[t].wait()
         c, first = t // tiles, t % tiles * LANES
@@ -334,6 +317,23 @@
 
     for t in range(tiles):
         fill(t)
+
+    beneath = lax.div(plane + last_plane, planes)
+    above = 1 - lax.div(plane + 2, planes) if planes > 2 else 0
+    pl.semaphore_wait(barrier, 1 + CORES * (beneath + above + row))
+
+    @pl.when(row == 1)
+    def _():
+        tell(row_in, plane, 1)
+
+    @pl.when((plane == last_plane) & (plane >= 1))
+    def _():
+        tell(last_in, plane - 1, 0)
+
+    @pl.when((plane >= 1) & (plane + 1 < last_plane))
+    def _():
+        tell(higher.at[2], plane - 1, 0)
+        tell(lower.at[2], plane + 1, 0)
 
     @pl.when(plane + 1 < last_plane)
     def _():

time: 60.6 us -> 60.6 us (level)
  no operation moved by 1% of the time
where the time goes in v5:
time: 60.6 us; the launch traced here: 60.5 us
  Pallas kernels  58.5 us (97%)
  between operations  1.93 us (3%)
    pallas_call x1, Pallas kernels, kernel_shards(): pl.pallas_call(functools.partial(kernel, n, chunks), out_shape=(out, out,...  57.3 us
    pallas_call x1, Pallas kernels, kernel_shards(): pl.pallas_call(functools.partial(write_out, gates - wide), out_shape=(out...  1.26 us

profile of v5, /device:TPU:0, one launch (start us, length us, event | category | flops | bytes accessed | tf_op | source)
XLA Modules:
  0.0 60.5 jit_solution(6195016337278493110)
XLA Ops:
  1.9 57.3 %shard_map.86 = (f32[256,768]{1,0:T(8,128)S(1)}, f32[256,768]{1,0:T(8,128)S(1)}, f32[8,768]{1,0:T(8,128)S(1)}, bf16[512,256]{1,0:T(8,128)(2,1)S(1)}, bf16[256,256]{1,0:T(8,128)(2,1)S(1)}) custom-call(f32[2,256,768]{2,1,0:T(8,128)} %x_any.1, s32[1]{0:T(128)S(6)} %copy.9.guard_any, s32[1]{0:T(128)S(6)} %copy.10.train_any, ...), custom_call_target="tpu_custom_call" | custom-call | flops 10000000000 | bytes 1572864 | tf_op jit(solution)/shard_map/pallas_call | solution.py:618
  59.2 1.3 %shard_map.87 = (f32[256,768]{1,0:T(8,128)}, f32[256,768]{1,0:T(8,128)}) custom-call(f32[256,768]{1,0:T(8,128)S(1)} %get-tuple-element.7.power_ref, f32[256,768]{1,0:T(8,128)S(1)} %get-tuple-element.8.total_ref, f32[8,768]{1,0:T(8,128)S(1)} %get-tuple-element.9.scale_ref, bf16[512,256]{1,0:T(8,128)(2,1)S(1)} %get-tuple-element.10.band_ref, ...), custom_call_target="tpu_custom_call" | custom-call | tf_op jit(solution)/shard_map/pallas_call | solution.py:655

commit v6 on v5

--- a/solution.py
+++ b/solution.py
@@ -367,12 +367,12 @@
 
     tell(row_known.at[1], plane, 1)
     hear(row_known.at[1])
+    send(plane, 1)
     for hop in (1, -1):
         @pl.when((plane + hop >= 0) & (plane + hop <= last_plane))
         def _():
             send(plane + hop, 1)
 
-    send(plane, 1)
     for k in range(2, planes):
         @pl.when(plane + k <= last_plane)
         def _():
@@ -391,6 +391,7 @@
             def _():
                 tell(lower.at[k + 1], plane + 1, 0)
 
+        tell(row_known.at[k], plane, 1)
         @pl.when(plane + k <= last_plane)
         def _():
             send(plane + k, 0)
@@ -399,7 +400,6 @@
         def _():
             send(plane - k, 0)
 
-        tell(row_known.at[k], plane, 1)
         hear(row_known.at[k])
         for hop in (k, -k):
             @pl.when((plane + hop >= 0) & (plane + hop <= last_plane))

time: 60.6 us -> 60.6 us (level)
  no operation moved by 1% of the time
where the time goes in v6:
time: 60.6 us; the launch traced here: 60.5 us
  Pallas kernels  58.5 us (97%)
  between operations  1.93 us (3%)
    pallas_call x1, Pallas kernels, kernel_shards(): pl.pallas_call(functools.partial(kernel, n, chunks), out_shape=(out, out,...  57.3 us
    pallas_call x1, Pallas kernels, kernel_shards(): pl.pallas_call(functools.partial(write_out, gates - wide), out_shape=(out...  1.26 us

profile of v6, /device:TPU:0, one launch (start us, length us, event | category | flops | bytes accessed | tf_op | source)
XLA Modules:
  0.0 60.5 jit_solution(2646353359481774334)
XLA Ops:
  1.9 57.3 %shard_map.86 = (f32[256,768]{1,0:T(8,128)S(1)}, f32[256,768]{1,0:T(8,128)S(1)}, f32[8,768]{1,0:T(8,128)S(1)}, bf16[512,256]{1,0:T(8,128)(2,1)S(1)}, bf16[256,256]{1,0:T(8,128)(2,1)S(1)}) custom-call(f32[2,256,768]{2,1,0:T(8,128)} %x_any.1, s32[1]{0:T(128)S(6)} %copy.9.guard_any, s32[1]{0:T(128)S(6)} %copy.10.train_any, ...), custom_call_target="tpu_custom_call" | custom-call | flops 10000000000 | bytes 1572864 | tf_op jit(solution)/shard_map/pallas_call | solution.py:618
  59.2 1.3 %shard_map.87 = (f32[256,768]{1,0:T(8,128)}, f32[256,768]{1,0:T(8,128)}) custom-call(f32[256,768]{1,0:T(8,128)S(1)} %get-tuple-element.7.power_ref, f32[256,768]{1,0:T(8,128)S(1)} %get-tuple-element.8.total_ref, f32[8,768]{1,0:T(8,128)S(1)} %get-tuple-element.9.scale_ref, bf16[512,256]{1,0:T(8,128)(2,1)S(1)} %get-tuple-element.10.band_ref, ...), custom_call_target="tpu_custom_call" | custom-call | tf_op jit(solution)/shard_map/pallas_call | solution.py:655

commit v7 on v5

--- a/solution.py
+++ b/solution.py
@@ -223,7 +223,7 @@
         (sin_any, twist_sin), (high_any, table_high), (low_any, table_low),
     ]
     loads = [pltpu.make_async_copy(*pair, load.at[i]) for i, pair in enumerate(loads)]
-    for copy in loads:
+    for copy in loads[:tiles]:
         copy.start()
     planes = n // PLANE
     last_plane = planes - 1
@@ -317,6 +317,8 @@
 
     for t in range(tiles):
         fill(t)
+    for copy in loads[tiles:]:
+        copy.start()
 
     beneath = lax.div(plane + last_plane, planes)
     above = 1 - lax.div(plane + 2, planes) if planes > 2 else 0

time: 60.6 us -> 60.6 us (level)
  no operation moved by 1% of the time
where the time goes in v7:
time: 60.6 us; the launch traced here: 60.5 us
  Pallas kernels  58.5 us (97%)
  between operations  1.93 us (3%)
    pallas_call x1, Pallas kernels, kernel_shards(): pl.pallas_call(functools.partial(kernel, n, chunks), out_shape=(out, out,...  57.3 us
    pallas_call x1, Pallas kernels, kernel_shards(): pl.pallas_call(functools.partial(write_out, gates - wide), out_shape=(out...  1.26 us

profile of v7, /device:TPU:0, one launch (start us, length us, event | category | flops | bytes accessed | tf_op | source)
XLA Modules:
  0.0 60.5 jit_solution(422493201341647921)
XLA Ops:
  1.9 57.3 %shard_map.86 = (f32[256,768]{1,0:T(8,128)S(1)}, f32[256,768]{1,0:T(8,128)S(1)}, f32[8,768]{1,0:T(8,128)S(1)}, bf16[512,256]{1,0:T(8,128)(2,1)S(1)}, bf16[256,256]{1,0:T(8,128)(2,1)S(1)}) custom-call(f32[2,256,768]{2,1,0:T(8,128)} %x_any.1, s32[1]{0:T(128)S(6)} %copy.9.guard_any, s32[1]{0:T(128)S(6)} %copy.10.train_any, ...), custom_call_target="tpu_custom_call" | custom-call | flops 10000000000 | bytes 1572864 | tf_op jit(solution)/shard_map/pallas_call | solution.py:620
  59.2 1.3 %shard_map.87 = (f32[256,768]{1,0:T(8,128)}, f32[256,768]{1,0:T(8,128)}) custom-call(f32[256,768]{1,0:T(8,128)S(1)} %get-tuple-element.7.power_ref, f32[256,768]{1,0:T(8,128)S(1)} %get-tuple-element.8.total_ref, f32[8,768]{1,0:T(8,128)S(1)} %get-tuple-element.9.scale_ref, bf16[512,256]{1,0:T(8,128)(2,1)S(1)} %get-tuple-element.10.band_ref, ...), custom_call_target="tpu_custom_call" | custom-call | tf_op jit(solution)/shard_map/pallas_call | solution.py:657
